TPU v7x, 32 devices: a whole 2x2x4 slice. The times are simulated.
32 devices in a mesh: depth: 4 (over y, x), screen: 8 (over z, core).
Axes of the slice: x: 2, y: 2, z: 4, core: 2. Of those that a mesh axis runs over, the one named last changes fastest.
Arguments:
- voxel_bins: int32 [32, 256, 2048], P('depth', None, 'screen'), may hold values from 0 to 255
- colors: bfloat16 [3, 256], replicated, may hold values from 0 to 2
- opacity: bfloat16 [256], replicated, may hold values from 0 to 1
- slab_order: int32 [8, 4], replicated, may hold values from 0 to 3, each once within a row
Outputs:
- image: float32 [4, 256, 2048], P(None, ('depth', 'screen'))
Inputs may be any that keep to these rules, and one draw needn't show every extreme that they name: `slab_order`: every row is a permutation of 0 to 3.
All inputs are finite; a program needn't handle non-finite values.
Results may differ from a plain program's by a relative error of at most 0.0003.
Values sent between devices are 32-bit elements; how exact they have to be, the bound alone decides.
No kernel may reach another device: no remote copies, remote signals or barrier semaphores. Data moves between devices by JAX's collectives and lax.ppermute only.
A program may use at most 64 MiB of HBM per device.

v0:
```python
import math
import jax
import jax.numpy as jnp
from jax import lax
from jax.sharding import PartitionSpec as P

low_count = 16
extinction = 3.0


def look_up(table_rows, bin_block):
    high_count = table_rows.shape[0] // 4
    low_part = bin_block % low_count
    high_part = bin_block // low_count
    low_onehot = (low_part[None, :] == jnp.arange(low_count, dtype=jnp.int32)[:, None]).astype(
        jnp.bfloat16
    )
    picked = jnp.dot(table_rows, low_onehot, preferred_element_type=jnp.float32)
    picked = picked.reshape(4, high_count, bin_block.shape[0])
    high_match = high_part[None, :] == jnp.arange(high_count, dtype=jnp.int32)[:, None]
    return jnp.sum(jnp.where(high_match[None], picked, 0.0), axis=1)


def render(voxel_bins, table_rows, total_samples):
    samples_here, row_count, col_count = voxel_bins.shape
    pixels = row_count * col_count
    per_step = math.gcd(samples_here, max(1, 131072 // pixels))
    blocks = voxel_bins.reshape(samples_here // per_step, per_step * pixels)
    extinct_rate = extinction / total_samples

    def advance(carried, bin_block):
        passed, color_sum = carried
        values = look_up(table_rows, bin_block).reshape(4, per_step, pixels)
        density = values[3]
        before = jnp.cumsum(density, axis=0) - density
        weight = (1.0 - jnp.exp(-extinct_rate * density)) * jnp.exp(
            -extinct_rate * (passed[None] + before)
        )
        color_sum = color_sum + jnp.sum(weight[None] * values[:3], axis=1)
        return ((passed + jnp.sum(density, axis=0), color_sum), None)

    start = (jnp.zeros((pixels,), jnp.float32), jnp.zeros((3, pixels), jnp.float32))
    (passed, color_sum), ignored = lax.scan(advance, start, blocks)
    final_alpha = 1.0 - jnp.exp(-extinct_rate * passed)
    partial_value = jnp.concatenate([color_sum, final_alpha[None]], axis=0)
    return partial_value.reshape(4, row_count, col_count)


def composite(pieces, places):
    in_front = (places[:, None, :] < places[:, :, None]).astype(jnp.float32)
    clear_log = jnp.log1p(-pieces[:, :, 3])
    front_log = jnp.einsum("tij,jtrw->itrw", in_front, clear_log, precision=lax.Precision.HIGHEST)
    shaded = jnp.sum(pieces[:, :, :3] * jnp.exp(front_log)[:, :, None], axis=0)
    total_alpha = 1.0 - jnp.exp(jnp.sum(clear_log, axis=0))
    merged = jnp.concatenate([shaded, total_alpha[:, None]], axis=1)
    return jnp.transpose(merged, (1, 2, 0, 3))


def local(voxel_bins, colors, opacity, slab_order):
    table = jnp.concatenate([colors, opacity[None]], axis=0)
    table_rows = table.reshape(4 * (table.shape[1] // low_count), low_count)
    depth_count = lax.axis_size("depth")
    total_samples = voxel_bins.shape[0] * depth_count
    partial_value = render(voxel_bins, table_rows, total_samples)
    own_order = lax.dynamic_slice_in_dim(slab_order, lax.axis_index("screen"), 1, 0)
    tile_block = composite(
        lax.all_to_all(partial_value[None], "depth", split_axis=2, concat_axis=0, tiled=True)[
            :, None
        ],
        own_order,
    )[:, :, 0]
    result = lax.all_to_all(tile_block, "screen", split_axis=1, concat_axis=2, tiled=True)
    return result


def solution(mesh):
    placed = (P("depth", None, "screen"), P(), P(), P())
    return jax.shard_map(
        local,
        mesh=mesh,
        in_specs=placed,
        out_specs=P(None, ("depth", "screen"), None),
        check_vma=False,
    )
```

profile of v0, /device:TPU:0, one launch (start us, length us, event | category | flops | bytes accessed | tf_op | source)
XLA Modules:
  0.0 185.4 jit_solution(1392531687887182417)
XLA Ops:
  0.0 4.0 %reshape.163 = s32[4,131072]{1,0:T(4,128)} reshape(s32[8,256,256]{2,1,0:T(8,128)} %param.6) | data formatting | bytes 4194304 | tf_op jit(solution)/shard_map/reshape | solution.py:28
  4.2 141.1 %while.15 = (s32[]{:T(128)}, f32[65536]{0:T(1024)}, f32[3,65536]{1,0:T(4,128)}, s32[4,131072]{1,0:T(4,128)}, bf16[64,16]{0,1:T(8,128)(2,1)S(1)}, /*index=5*/s32[]{:T(128)}, f32[]{:T(128)}, s32[]{:T(128)}) while((s32[]{:T(128)}, f32[65536]{0:T(1024)}, f32[3,65536]{1,0:T(4,128)}, s32[4,131072]{1,0:T(4,128)}, ...), condition=%wide.region_5.6_spmd.clone, body=%wide.region_0.5_spmd.clone.sunk | while | flops 293994496 | bytes 31983784 | solution.py:43
  4.2 3.4 %and_select_fusion.4 = (s32[1,131072]{1,0:T(1,128)S(1)}, s32[1,131072]{1,0:T(1,128)S(1)}) fusion(s32[4,131072]{1,0:T(4,128)} %get-tuple-element.186, s32[]{:T(128)} %get-tuple-element.175), kind=kLoop, calls=%fused_computation.5.clone.1 | loop fusion | flops 1441792 | bytes 1572868 | tf_op jit(solution)/shard_map/while/body/eval_jaxpr/jit(remainder)/select_n | solution.py:13
  7.6 3.8 %and_select_fusion.5 = s32[1,131072]{1,0:T(1,128)S(1)} fusion(s32[1,131072]{1,0:T(1,128)S(1)} %get-tuple-element.163, s32[4,131072]{1,0:T(4,128)} %get-tuple-element.186, s32[]{:T(128)} %get-tuple-element.175), kind=kLoop, calls=%fused_computation.6.clone.1 | loop fusion | flops 1572864 | bytes 1572868 | tf_op jit(solution)/shard_map/while/body/eval_jaxpr/jit(floor_divide)/jit(_where)/select_n | solution.py:14
  11.4 1.1 iota_compare_fusion.4
  12.5 11.0 %select_reduce_fusion.2 = f32[4,131072]{1,0:T(4,128)S(1)} fusion(pred[16,131072]{1,0:T(8,128)(4,1)S(1)} %iota_compare_fusion.4, bf16[64,16]{0,1:T(8,128)(2,1)S(1)} %get-tuple-element.187, s32[131072]{0:T(1024)S(1)} %bitcast.47), kind=kOutput, calls=%fused_computation.clone.1 | convolution fusion | flops 286785536 | bytes 4720640 | tf_op jit(solution)/shard_map/while/body/eval_jaxpr/dot_general | solution.py:18
  23.5 1.6 slice_reduce_fusion.2
  25.4 0.6 reduce_sum.71
  26.0 0.8 fusion.17
  26.8 1.8 reduce_window_sum.13
  28.7 1.8 exponential_multiply_fusion.2
  30.5 2.9 %slice.46 = f32[3,2,65536]{2,1,0:T(2,128)} reshape(f32[3,131072]{1,0:T(4,128)S(1)} %bitcast.45) | data formatting | bytes 3145728 | tf_op jit(solution)/shard_map/while/body/eval_jaxpr/slice | solution.py:39
  33.3 3.9 %multiply_reduce_fusion.2 = f32[3,65536]{1,0:T(4,128)S(1)} fusion(f32[3,2,65536]{2,1,0:T(2,128)} %slice.46, f32[2,65536]{1,0:T(2,128)S(1)} %exponential_multiply_fusion.2), kind=kLoop, calls=%fused_computation.7.clone.1 | loop fusion | flops 589824 | bytes 2883584 | tf_op jit(solution)/shard_map/while/body/eval_jaxpr/reduce_sum | solution.py:39
  37.2 0.6 select_add_fusion.2
  37.9 0.9 copy-done.2
  38.8 3.4 %and_select_fusion.4 = (s32[1,131072]{1,0:T(1,128)S(1)}, s32[1,131072]{1,0:T(1,128)S(1)}) fusion(s32[4,131072]{1,0:T(4,128)} %get-tuple-element.186, s32[]{:T(128)} %get-tuple-element.175), kind=kLoop, calls=%fused_computation.5.clone.1 | loop fusion | flops 1441792 | bytes 1572868 | tf_op jit(solution)/shard_map/while/body/eval_jaxpr/jit(remainder)/select_n | solution.py:13
  42.2 3.8 %and_select_fusion.5 = s32[1,131072]{1,0:T(1,128)S(1)} fusion(s32[1,131072]{1,0:T(1,128)S(1)} %get-tuple-element.163, s32[4,131072]{1,0:T(4,128)} %get-tuple-element.186, s32[]{:T(128)} %get-tuple-element.175), kind=kLoop, calls=%fused_computation.6.clone.1 | loop fusion | flops 1572864 | bytes 1572868 | tf_op jit(solution)/shard_map/while/body/eval_jaxpr/jit(floor_divide)/jit(_where)/select_n | solution.py:14
  45.9 1.1 iota_compare_fusion.4
  47.0 11.0 %select_reduce_fusion.2 = f32[4,131072]{1,0:T(4,128)S(1)} fusion(pred[16,131072]{1,0:T(8,128)(4,1)S(1)} %iota_compare_fusion.4, bf16[64,16]{0,1:T(8,128)(2,1)S(1)} %get-tuple-element.187, s32[131072]{0:T(1024)S(1)} %bitcast.47), kind=kOutput, calls=%fused_computation.clone.1 | convolution fusion | flops 286785536 | bytes 4720640 | tf_op jit(solution)/shard_map/while/body/eval_jaxpr/dot_general | solution.py:18
  58.1 1.6 slice_reduce_fusion.2
  60.0 0.6 reduce_sum.71
  60.6 1.7 fusion.17
  62.3 1.8 reduce_window_sum.13
  64.2 1.8 exponential_multiply_fusion.2
  66.0 2.9 %slice.46 = f32[3,2,65536]{2,1,0:T(2,128)} reshape(f32[3,131072]{1,0:T(4,128)S(1)} %bitcast.45) | data formatting | bytes 3145728 | tf_op jit(solution)/shard_map/while/body/eval_jaxpr/slice | solution.py:39
  68.8 3.9 %multiply_reduce_fusion.2 = f32[3,65536]{1,0:T(4,128)S(1)} fusion(f32[3,2,65536]{2,1,0:T(2,128)} %slice.46, f32[2,65536]{1,0:T(2,128)S(1)} %exponential_multiply_fusion.2), kind=kLoop, calls=%fused_computation.7.clone.1 | loop fusion | flops 589824 | bytes 2883584 | tf_op jit(solution)/shard_map/while/body/eval_jaxpr/reduce_sum | solution.py:39
  72.7 0.6 select_add_fusion.2
  73.4 0.9 copy-done.2
  74.3 3.4 %and_select_fusion.4 = (s32[1,131072]{1,0:T(1,128)S(1)}, s32[1,131072]{1,0:T(1,128)S(1)}) fusion(s32[4,131072]{1,0:T(4,128)} %get-tuple-element.186, s32[]{:T(128)} %get-tuple-element.175), kind=kLoop, calls=%fused_computation.5.clone.1 | loop fusion | flops 1441792 | bytes 1572868 | tf_op jit(solution)/shard_map/while/body/eval_jaxpr/jit(remainder)/select_n | solution.py:13
  77.7 3.8 %and_select_fusion.5 = s32[1,131072]{1,0:T(1,128)S(1)} fusion(s32[1,131072]{1,0:T(1,128)S(1)} %get-tuple-element.163, s32[4,131072]{1,0:T(4,128)} %get-tuple-element.186, s32[]{:T(128)} %get-tuple-element.175), kind=kLoop, calls=%fused_computation.6.clone.1 | loop fusion | flops 1572864 | bytes 1572868 | tf_op jit(solution)/shard_map/while/body/eval_jaxpr/jit(floor_divide)/jit(_where)/select_n | solution.py:14
  81.4 1.1 iota_compare_fusion.4
  82.5 11.0 %select_reduce_fusion.2 = f32[4,131072]{1,0:T(4,128)S(1)} fusion(pred[16,131072]{1,0:T(8,128)(4,1)S(1)} %iota_compare_fusion.4, bf16[64,16]{0,1:T(8,128)(2,1)S(1)} %get-tuple-element.187, s32[131072]{0:T(1024)S(1)} %bitcast.47), kind=kOutput, calls=%fused_computation.clone.1 | convolution fusion | flops 286785536 | bytes 4720640 | tf_op jit(solution)/shard_map/while/body/eval_jaxpr/dot_general | solution.py:18
  93.6 1.6 slice_reduce_fusion.2
  95.5 0.6 reduce_sum.71
  96.1 1.7 fusion.17
  97.8 1.8 reduce_window_sum.13
  99.7 1.8 exponential_multiply_fusion.2
  101.5 2.9 %slice.46 = f32[3,2,65536]{2,1,0:T(2,128)} reshape(f32[3,131072]{1,0:T(4,128)S(1)} %bitcast.45) | data formatting | bytes 3145728 | tf_op jit(solution)/shard_map/while/body/eval_jaxpr/slice | solution.py:39
  104.3 3.9 %multiply_reduce_fusion.2 = f32[3,65536]{1,0:T(4,128)S(1)} fusion(f32[3,2,65536]{2,1,0:T(2,128)} %slice.46, f32[2,65536]{1,0:T(2,128)S(1)} %exponential_multiply_fusion.2), kind=kLoop, calls=%fused_computation.7.clone.1 | loop fusion | flops 589824 | bytes 2883584 | tf_op jit(solution)/shard_map/while/body/eval_jaxpr/reduce_sum | solution.py:39
  108.2 0.6 select_add_fusion.2
  108.9 0.9 copy-done.2
  109.8 3.4 %and_select_fusion.4 = (s32[1,131072]{1,0:T(1,128)S(1)}, s32[1,131072]{1,0:T(1,128)S(1)}) fusion(s32[4,131072]{1,0:T(4,128)} %get-tuple-element.186, s32[]{:T(128)} %get-tuple-element.175), kind=kLoop, calls=%fused_computation.5.clone.1 | loop fusion | flops 1441792 | bytes 1572868 | tf_op jit(solution)/shard_map/while/body/eval_jaxpr/jit(remainder)/select_n | solution.py:13
  113.2 3.8 %and_select_fusion.5 = s32[1,131072]{1,0:T(1,128)S(1)} fusion(s32[1,131072]{1,0:T(1,128)S(1)} %get-tuple-element.163, s32[4,131072]{1,0:T(4,128)} %get-tuple-element.186, s32[]{:T(128)} %get-tuple-element.175), kind=kLoop, calls=%fused_computation.6.clone.1 | loop fusion | flops 1572864 | bytes 1572868 | tf_op jit(solution)/shard_map/while/body/eval_jaxpr/jit(floor_divide)/jit(_where)/select_n | solution.py:14
  116.9 1.1 iota_compare_fusion.4
  118.0 11.0 %select_reduce_fusion.2 = f32[4,131072]{1,0:T(4,128)S(1)} fusion(pred[16,131072]{1,0:T(8,128)(4,1)S(1)} %iota_compare_fusion.4, bf16[64,16]{0,1:T(8,128)(2,1)S(1)} %get-tuple-element.187, s32[131072]{0:T(1024)S(1)} %bitcast.47), kind=kOutput, calls=%fused_computation.clone.1 | convolution fusion | flops 286785536 | bytes 4720640 | tf_op jit(solution)/shard_map/while/body/eval_jaxpr/dot_general | solution.py:18
  129.1 1.6 slice_reduce_fusion.2
  131.0 0.6 reduce_sum.71
  131.6 1.7 fusion.17
  133.3 1.8 reduce_window_sum.13
  135.2 1.8 exponential_multiply_fusion.2
  137.0 2.9 %slice.46 = f32[3,2,65536]{2,1,0:T(2,128)} reshape(f32[3,131072]{1,0:T(4,128)S(1)} %bitcast.45) | data formatting | bytes 3145728 | tf_op jit(solution)/shard_map/while/body/eval_jaxpr/slice | solution.py:39
  139.8 3.9 %multiply_reduce_fusion.2 = f32[3,65536]{1,0:T(4,128)S(1)} fusion(f32[3,2,65536]{2,1,0:T(2,128)} %slice.46, f32[2,65536]{1,0:T(2,128)S(1)} %exponential_multiply_fusion.2), kind=kLoop, calls=%fused_computation.7.clone.1 | loop fusion | flops 589824 | bytes 2883584 | tf_op jit(solution)/shard_map/while/body/eval_jaxpr/reduce_sum | solution.py:39
  143.7 0.6 select_add_fusion.2
  144.4 0.9 copy-done.2
  145.3 1.0 exponential_subtract_fusion
  146.3 2.7 %pad_maximum_fusion = f32[1,4,256,256]{3,1,0,2:T(4,128)} fusion(f32[1,1,256,256]{3,1,0,2:T(1,128)S(1)} %bitcast.53, f32[1,3,256,256]{3,1,0,2:T(4,128)} %bitcast.48), kind=kLoop, calls=%fused_computation.17 | loop fusion | flops 262144 | bytes 2097152 | tf_op jit(solution)/shard_map/concatenate | solution.py:45
  149.0 5.2 %all-to-all-start = ((f32[1,4,256,256]{3,1,0,2:T(4,128)}), f32[1,4,256,256]{3,1,0,2:T(4,128)S(1)}, u32[]{:S(2)}, u32[]{:S(2)}) async-start(f32[1,4,256,256]{3,1,0,2:T(4,128)} %pad_maximum_fusion), calls=%async_computation | async-start | bytes 2097152 | tf_op jit(solution)/shard_map/all_to_all | solution.py:67
  154.4 13.4 %all-to-all-done = f32[1,4,256,256]{3,1,0,2:T(4,128)S(1)} async-done(((f32[1,4,256,256]{3,1,0,2:T(4,128)}), f32[1,4,256,256]{3,1,0,2:T(4,128)S(1)}, u32[]{:S(2)}, u32[]{:S(2)}) %all-to-all-start) | async-done | bytes 1048608 | tf_op jit(solution)/shard_map/all_to_all | solution.py:67
  167.8 0.7 copy.24
  168.5 0.3 fusion.6
  168.8 0.6 fusion.2
  169.4 0.5 fusion.3
  170.2 14.4 %all_to_all.33 = f32[4,64,256]{2,0,1:T(4,128)S(1)} all-to-all(f32[4,64,256]{2,0,1:T(4,128)S(1)} %copy.19), channel_id=1, replica_groups=mesh['depth'=4,'screen'=8] {'screen'}, dimensions={1} | all-to-all | bytes 524288 | tf_op jit(solution)/shard_map/all_to_all | solution.py:72
  184.6 0.8 copy.20
  (32 shorter events, 1.9 us)
Async XLA Ops:
  0.0 154.2 %copy-start = (s32[8,4]{0,1:T(4,128)S(1)}, s32[8,4]{0,1:T(4,128)}, u32[]{:S(2)}) copy-start(s32[8,4]{0,1:T(4,128)} %param.9) | copy-start | bytes 388
  0.0 4.0 %copy-start.4 = (bf16[256]{0:T(256)(128)(2,1)S(1)}, bf16[256]{0:T(256)(128)(2,1)}, u32[]{:S(2)}) copy-start(bf16[256]{0:T(256)(128)(2,1)} %param.8) | copy-start | bytes 1540
  0.0 4.0 %copy-start.3 = (bf16[3,256]{1,0:T(4,128)(2,1)S(1)}, bf16[3,256]{1,0:T(4,128)(2,1)}, u32[]{:S(2)}) copy-start(bf16[3,256]{1,0:T(4,128)(2,1)} %param.7) | copy-start | bytes 4612
  33.3 3.9 %copy-start.1 = (f32[3,65536]{1,0:T(4,128)S(1)}, f32[3,65536]{1,0:T(4,128)}, u32[]{:S(2)}) copy-start(f32[3,65536]{1,0:T(4,128)} %get-tuple-element.177) | copy-start | bytes 2359300 | tf_op jit(solution)/shard_map/while
  37.8 1.0 copy-start.2
  68.8 3.9 %copy-start.1 = (f32[3,65536]{1,0:T(4,128)S(1)}, f32[3,65536]{1,0:T(4,128)}, u32[]{:S(2)}) copy-start(f32[3,65536]{1,0:T(4,128)} %get-tuple-element.177) | copy-start | bytes 2359300 | tf_op jit(solution)/shard_map/while
  73.4 1.0 copy-start.2
  104.3 3.9 %copy-start.1 = (f32[3,65536]{1,0:T(4,128)S(1)}, f32[3,65536]{1,0:T(4,128)}, u32[]{:S(2)}) copy-start(f32[3,65536]{1,0:T(4,128)} %get-tuple-element.177) | copy-start | bytes 2359300 | tf_op jit(solution)/shard_map/while
  108.9 1.0 copy-start.2
  139.8 3.9 %copy-start.1 = (f32[3,65536]{1,0:T(4,128)S(1)}, f32[3,65536]{1,0:T(4,128)}, u32[]{:S(2)}) copy-start(f32[3,65536]{1,0:T(4,128)} %get-tuple-element.177) | copy-start | bytes 2359300 | tf_op jit(solution)/shard_map/while
  144.4 1.0 copy-start.2
  149.0 18.8 %all-to-all-start = ((f32[1,4,256,256]{3,1,0,2:T(4,128)}), f32[1,4,256,256]{3,1,0,2:T(4,128)S(1)}, u32[]{:S(2)}, u32[]{:S(2)}) async-start(f32[1,4,256,256]{3,1,0,2:T(4,128)} %pad_maximum_fusion), calls=%async_computation | async-start | bytes 2097152 | tf_op jit(solution)/shard_map/all_to_all | solution.py:67
where the time goes:
time: 186 us; the launch traced here: 185 us
  other arithmetic  78.4 us (42%)
  matrix products  44.8 us (24%)
  local copies, waits for them, and re-layouts  28.7 us (15%)
  blocking collectives  14.4 us (8%)
  waiting for transfers between devices  13.4 us (7%)
  starting transfers between devices  5.19 us (3%)
    dot_general x4, matrix products, look_up(): picked = jnp.dot(table_rows, low_onehot, preferred_element_type=jnp.float32)  44.2 us
    reduce_sum x4, other arithmetic, advance(): color_sum = color_sum + jnp.sum(weight[None] * values[:3], axis=1)  15.5 us
    select_n x4, other arithmetic, look_up(): high_part = bin_block // low_count  15 us
    all_to_all x1, blocking collectives, local(): lax.all_to_all(tile_block, 'screen', split_axis=1, concat_axis=2, tiled=T...  14.4 us
    select_n x4, other arithmetic, look_up(): low_part = bin_block % low_count  13.5 us
    all_to_all x1, waiting for transfers between devices, local(): lax.all_to_all(partial_value[None], 'depth', split_axis=2, concat_axis=0,...  13.4 us
    slice x4, local copies, waits for them, and re-layouts, advance(): color_sum = color_sum + jnp.sum(weight[None] * values[:3], axis=1)  11.4 us
    another operation x4, other arithmetic, advance(): before = jnp.cumsum(density, axis=0) - density  7.29 us
  transfers between devices with their start and end apart: 1, of which 1 were waited for; matrix products, arithmetic and copies ran while one was open for 0% of the time, Pallas kernels for 0%

commit v1 on v0

--- a/solution.py
+++ b/solution.py
@@ -3,9 +3,29 @@
 import jax.numpy as jnp
 from jax import lax
 from jax.sharding import PartitionSpec as P
+from jax.lax import axis_index, axis_size, ppermute
 
 low_count = 16
 extinction = 3.0
+
+
+def _trace_words(mat, ndim_at, vector):
+    n_now = mat.shape
+    w1 = jnp.moveaxis(
+        mat.reshape(*n_now[:ndim_at], vector, n_now[ndim_at] // vector, *n_now[ndim_at + 1 :]),
+        ndim_at,
+        0,
+    )
+    return w1
+
+
+def press_rounds(mine, which_dim):
+    mine = jnp.moveaxis(mine, 0, which_dim)
+    k_now = mine.shape
+    tmp = mine.reshape(
+        *k_now[:which_dim], k_now[which_dim] * k_now[which_dim + 1], *k_now[which_dim + 2 :]
+    )
+    return tmp
 
 
 def look_up(table_rows, bin_block):
@@ -69,7 +89,26 @@
         ],
         own_order,
     )[:, :, 0]
-    result = lax.all_to_all(tile_block, "screen", split_axis=1, concat_axis=2, tiled=True)
+
+    def create_leaves(incoming_x, which_axis, local_x, chunk):
+        m_next, state_next = (axis_size(which_axis), axis_index(which_axis))
+        h_now = _trace_words(incoming_x, local_x, m_next)
+        v_next = h_now
+        j = 1
+        while j < m_next:
+            upper, z2 = ((state_next + j) % m_next, (state_next - j) % m_next)
+            y_new = lax.dynamic_index_in_dim(h_now, upper, 0)
+            block_out = ppermute(
+                y_new,
+                axis_name=which_axis,
+                perm=[(num, (num + j) % m_next) for num in range(m_next)],
+            )
+            v_next = lax.dynamic_update_slice_in_dim(v_next, block_out, z2, axis=0)
+            j += 1
+        vec_out = press_rounds(v_next, chunk)
+        return vec_out
+
+    result = create_leaves(tile_block, "screen", 1, 2)
     return result
 
 

time: 186 us -> 150 us (0.81)
  other arithmetic: 78.4 us -> 47.5 us
  blocking collectives: 14.4 us -> 0 us
  starting transfers between devices: 5.19 us -> 14.7 us
    all_to_all x1 -> x0, blocking collectives: 14.4 us -> none  [local(): lax.all_to_all(tile_block, 'screen', split_axis=1, concat_axis=2, tiled=T...]
    ppermute x0 -> x7, starting transfers between devices: none -> 9.49 us  [create_leaves(): ppermute(y_new, axis_name=which_axis, perm=[(num, (num + j) % m_next) for...]
    select_n x4, other arithmetic: 13.5 us -> 7.1 us  [look_up(): low_part = bin_block % low_count]
    select_n x4, other arithmetic: 15 us -> 8.8 us  [look_up(): high_part = bin_block // low_count]
    add x4, other arithmetic: 5.98 us -> 0.28 us  [advance(): return ((passed + jnp.sum(density, axis=0), color_sum), None)]
    mul x4, other arithmetic: 7.29 us -> 2.88 us  [advance(): (1.0 - jnp.exp(-extinct_rate * density)) * jnp.exp(-extinct_rate * (passe...]
    reduce_sum x4, other arithmetic: 15.5 us -> 11.2 us  [advance(): color_sum = color_sum + jnp.sum(weight[None] * values[:3], axis=1)]
    another operation x4, other arithmetic: 7.29 us -> 4.24 us  [advance(): before = jnp.cumsum(density, axis=0) - density]
  transfers between devices with their start and end apart: 1 -> 8, of which waited for: 1 -> 3; matrix products, arithmetic and copies ran while one was open for 0% -> 0% of each run, Pallas kernels for 0% -> 0%
where the time goes in v1:
time: 150 us
  other arithmetic  47.5 us (32%)
  matrix products  44.8 us (30%)
  local copies, waits for them, and re-layouts  27.3 us (18%)
  waiting for transfers between devices  14.9 us (10%)
  starting transfers between devices  14.7 us (10%)
    dot_general x4, matrix products, look_up(): picked = jnp.dot(table_rows, low_onehot, preferred_element_type=jnp.float32)  44.2 us
    all_to_all x1, waiting for transfers between devices, local(): lax.all_to_all(partial_value[None], 'depth', split_axis=2, concat_axis=0,...  13.4 us
    slice x4, local copies, waits for them, and re-layouts, advance(): color_sum = color_sum + jnp.sum(weight[None] * values[:3], axis=1)  11.4 us
    reduce_sum x4, other arithmetic, advance(): color_sum = color_sum + jnp.sum(weight[None] * values[:3], axis=1)  11.2 us
    ppermute x7, starting transfers between devices, create_leaves(): ppermute(y_new, axis_name=which_axis, perm=[(num, (num + j) % m_next) for...  9.49 us
    select_n x4, other arithmetic, look_up(): high_part = bin_block // low_count  8.8 us
    select_n x4, other arithmetic, look_up(): low_part = bin_block % low_count  7.1 us
    slice x4, local copies, waits for them, and re-layouts, advance(): density = values[3]  6.27 us
  transfers between devices with their start and end apart: 8, of which 3 were waited for; matrix products, arithmetic and copies ran while one was open for 0% of the time, Pallas kernels for 0%

profile of v1, /device:TPU:0, one launch (start us, length us, event | category | flops | bytes accessed | tf_op | source)
XLA Modules:
  0.0 149.8 jit_solution(13506434463822965748)
XLA Ops:
  0.0 2.7 %reshape.180 = s32[4,131072]{1,0:T(4,128)S(1)} reshape(s32[8,256,256]{2,1,0:T(8,128)} %param.6) | data formatting | bytes 4194304 | tf_op jit(solution)/shard_map/reshape | solution.py:48
  2.9 111.3 %while.15 = (s32[]{:T(128)}, f32[65536]{0:T(1024)S(1)}, f32[3,65536]{1,0:T(4,128)}, s32[4,131072]{1,0:T(4,128)S(1)}, bf16[64,16]{0,1:T(8,128)(2,1)S(1)}, /*index=5*/s32[]{:T(128)}, f32[]{:T(128)}, s32[]{:T(128)}) while((s32[]{:T(128)}, f32[65536]{0:T(1024)S(1)}, f32[3,65536]{1,0:T(4,128)}, s32[4,131072]{1,0:T(4,128)S(1)}, ...), condition=%wide.region_5.6_spmd.clone, body=%wide.region_0.5_spmd.clone.sunk | while | flops 293994496 | bytes 55052548 | solution.py:63
  2.9 1.8 %and_select_fusion.4 = (s32[1,131072]{1,0:T(1,128)S(1)}, s32[1,131072]{1,0:T(1,128)S(1)}) fusion(s32[4,131072]{1,0:T(4,128)S(1)} %get-tuple-element.187, s32[]{:T(128)S(6)} %copy.20), kind=kLoop, calls=%fused_computation.5.clone.1 | loop fusion | flops 1441792 | bytes 1572868 | tf_op jit(solution)/shard_map/while/body/eval_jaxpr/jit(remainder)/select_n | solution.py:33
  4.7 2.2 %and_select_fusion.5 = s32[1,131072]{1,0:T(1,128)S(1)} fusion(s32[1,131072]{1,0:T(1,128)S(1)} %get-tuple-element.164, s32[4,131072]{1,0:T(4,128)S(1)} %get-tuple-element.187, s32[]{:T(128)S(6)} %copy.20), kind=kLoop, calls=%fused_computation.6.clone.1 | loop fusion | flops 1572864 | bytes 1572868 | tf_op jit(solution)/shard_map/while/body/eval_jaxpr/jit(floor_divide)/jit(_where)/select_n | solution.py:34
  6.9 1.1 iota_compare_fusion.4
  8.0 11.0 %select_reduce_fusion.2 = f32[4,131072]{1,0:T(4,128)S(1)} fusion(pred[16,131072]{1,0:T(8,128)(4,1)S(1)} %iota_compare_fusion.4, bf16[64,16]{0,1:T(8,128)(2,1)S(1)} %get-tuple-element.188, s32[131072]{0:T(1024)S(1)} %bitcast.60), kind=kOutput, calls=%fused_computation.clone.1 | convolution fusion | flops 286785536 | bytes 4720640 | tf_op jit(solution)/shard_map/while/body/eval_jaxpr/dot_general | solution.py:38
  19.0 1.6 %slice_reduce_fusion.2 = f32[131072]{0:T(1024)S(1)} fusion(f32[4,131072]{1,0:T(4,128)S(1)} %select_reduce_fusion.2), kind=kLoop, calls=%fused_computation.12.clone.1 | loop fusion | bytes 1048576 | tf_op jit(solution)/shard_map/while/body/eval_jaxpr/slice | solution.py:54
  20.9 0.6 reduce_sum.68
  21.6 2.9 %slice.46 = f32[3,2,65536]{2,1,0:T(2,128)} reshape(f32[3,131072]{1,0:T(4,128)S(1)} %bitcast.58) | data formatting | bytes 3145728 | tf_op jit(solution)/shard_map/while/body/eval_jaxpr/slice | solution.py:59
  24.5 1.1 reduce_window_sum.13
  25.6 0.7 exponential_multiply_fusion.2
  26.3 2.8 %multiply_reduce_fusion.2 = f32[3,65536]{1,0:T(4,128)S(1)} fusion(f32[3,2,65536]{2,1,0:T(2,128)S(1)} %copy-done.1, f32[2,65536]{1,0:T(2,128)S(1)} %exponential_multiply_fusion.2), kind=kLoop, calls=%fused_computation.7.clone.1 | loop fusion | flops 589824 | bytes 2883584 | tf_op jit(solution)/shard_map/while/body/eval_jaxpr/reduce_sum | solution.py:59
  29.1 0.6 select_add_fusion.2
  29.8 1.0 copy-done.3
  30.7 1.8 %and_select_fusion.4 = (s32[1,131072]{1,0:T(1,128)S(1)}, s32[1,131072]{1,0:T(1,128)S(1)}) fusion(s32[4,131072]{1,0:T(4,128)S(1)} %get-tuple-element.187, s32[]{:T(128)S(6)} %copy.20), kind=kLoop, calls=%fused_computation.5.clone.1 | loop fusion | flops 1441792 | bytes 1572868 | tf_op jit(solution)/shard_map/while/body/eval_jaxpr/jit(remainder)/select_n | solution.py:33
  32.5 2.2 %and_select_fusion.5 = s32[1,131072]{1,0:T(1,128)S(1)} fusion(s32[1,131072]{1,0:T(1,128)S(1)} %get-tuple-element.164, s32[4,131072]{1,0:T(4,128)S(1)} %get-tuple-element.187, s32[]{:T(128)S(6)} %copy.20), kind=kLoop, calls=%fused_computation.6.clone.1 | loop fusion | flops 1572864 | bytes 1572868 | tf_op jit(solution)/shard_map/while/body/eval_jaxpr/jit(floor_divide)/jit(_where)/select_n | solution.py:34
  34.7 1.1 iota_compare_fusion.4
  35.8 11.0 %select_reduce_fusion.2 = f32[4,131072]{1,0:T(4,128)S(1)} fusion(pred[16,131072]{1,0:T(8,128)(4,1)S(1)} %iota_compare_fusion.4, bf16[64,16]{0,1:T(8,128)(2,1)S(1)} %get-tuple-element.188, s32[131072]{0:T(1024)S(1)} %bitcast.60), kind=kOutput, calls=%fused_computation.clone.1 | convolution fusion | flops 286785536 | bytes 4720640 | tf_op jit(solution)/shard_map/while/body/eval_jaxpr/dot_general | solution.py:38
  46.9 1.6 %slice_reduce_fusion.2 = f32[131072]{0:T(1024)S(1)} fusion(f32[4,131072]{1,0:T(4,128)S(1)} %select_reduce_fusion.2), kind=kLoop, calls=%fused_computation.12.clone.1 | loop fusion | bytes 1048576 | tf_op jit(solution)/shard_map/while/body/eval_jaxpr/slice | solution.py:54
  48.8 0.6 reduce_sum.68
  49.5 2.9 %slice.46 = f32[3,2,65536]{2,1,0:T(2,128)} reshape(f32[3,131072]{1,0:T(4,128)S(1)} %bitcast.58) | data formatting | bytes 3145728 | tf_op jit(solution)/shard_map/while/body/eval_jaxpr/slice | solution.py:59
  52.3 1.1 reduce_window_sum.13
  53.4 0.7 exponential_multiply_fusion.2
  54.1 2.8 %multiply_reduce_fusion.2 = f32[3,65536]{1,0:T(4,128)S(1)} fusion(f32[3,2,65536]{2,1,0:T(2,128)S(1)} %copy-done.1, f32[2,65536]{1,0:T(2,128)S(1)} %exponential_multiply_fusion.2), kind=kLoop, calls=%fused_computation.7.clone.1 | loop fusion | flops 589824 | bytes 2883584 | tf_op jit(solution)/shard_map/while/body/eval_jaxpr/reduce_sum | solution.py:59
  57.0 0.6 select_add_fusion.2
  57.6 1.0 copy-done.3
  58.6 1.8 %and_select_fusion.4 = (s32[1,131072]{1,0:T(1,128)S(1)}, s32[1,131072]{1,0:T(1,128)S(1)}) fusion(s32[4,131072]{1,0:T(4,128)S(1)} %get-tuple-element.187, s32[]{:T(128)S(6)} %copy.20), kind=kLoop, calls=%fused_computation.5.clone.1 | loop fusion | flops 1441792 | bytes 1572868 | tf_op jit(solution)/shard_map/while/body/eval_jaxpr/jit(remainder)/select_n | solution.py:33
  60.3 2.2 %and_select_fusion.5 = s32[1,131072]{1,0:T(1,128)S(1)} fusion(s32[1,131072]{1,0:T(1,128)S(1)} %get-tuple-element.164, s32[4,131072]{1,0:T(4,128)S(1)} %get-tuple-element.187, s32[]{:T(128)S(6)} %copy.20), kind=kLoop, calls=%fused_computation.6.clone.1 | loop fusion | flops 1572864 | bytes 1572868 | tf_op jit(solution)/shard_map/while/body/eval_jaxpr/jit(floor_divide)/jit(_where)/select_n | solution.py:34
  62.5 1.1 iota_compare_fusion.4
  63.6 11.0 %select_reduce_fusion.2 = f32[4,131072]{1,0:T(4,128)S(1)} fusion(pred[16,131072]{1,0:T(8,128)(4,1)S(1)} %iota_compare_fusion.4, bf16[64,16]{0,1:T(8,128)(2,1)S(1)} %get-tuple-element.188, s32[131072]{0:T(1024)S(1)} %bitcast.60), kind=kOutput, calls=%fused_computation.clone.1 | convolution fusion | flops 286785536 | bytes 4720640 | tf_op jit(solution)/shard_map/while/body/eval_jaxpr/dot_general | solution.py:38
  74.7 1.6 %slice_reduce_fusion.2 = f32[131072]{0:T(1024)S(1)} fusion(f32[4,131072]{1,0:T(4,128)S(1)} %select_reduce_fusion.2), kind=kLoop, calls=%fused_computation.12.clone.1 | loop fusion | bytes 1048576 | tf_op jit(solution)/shard_map/while/body/eval_jaxpr/slice | solution.py:54
  76.6 0.6 reduce_sum.68
  77.3 2.9 %slice.46 = f32[3,2,65536]{2,1,0:T(2,128)} reshape(f32[3,131072]{1,0:T(4,128)S(1)} %bitcast.58) | data formatting | bytes 3145728 | tf_op jit(solution)/shard_map/while/body/eval_jaxpr/slice | solution.py:59
  80.1 1.1 reduce_window_sum.13
  81.2 0.7 exponential_multiply_fusion.2
  82.0 2.8 %multiply_reduce_fusion.2 = f32[3,65536]{1,0:T(4,128)S(1)} fusion(f32[3,2,65536]{2,1,0:T(2,128)S(1)} %copy-done.1, f32[2,65536]{1,0:T(2,128)S(1)} %exponential_multiply_fusion.2), kind=kLoop, calls=%fused_computation.7.clone.1 | loop fusion | flops 589824 | bytes 2883584 | tf_op jit(solution)/shard_map/while/body/eval_jaxpr/reduce_sum | solution.py:59
  84.8 0.6 select_add_fusion.2
  85.4 1.0 copy-done.3
  86.4 1.8 %and_select_fusion.4 = (s32[1,131072]{1,0:T(1,128)S(1)}, s32[1,131072]{1,0:T(1,128)S(1)}) fusion(s32[4,131072]{1,0:T(4,128)S(1)} %get-tuple-element.187, s32[]{:T(128)S(6)} %copy.20), kind=kLoop, calls=%fused_computation.5.clone.1 | loop fusion | flops 1441792 | bytes 1572868 | tf_op jit(solution)/shard_map/while/body/eval_jaxpr/jit(remainder)/select_n | solution.py:33
  88.2 2.2 %and_select_fusion.5 = s32[1,131072]{1,0:T(1,128)S(1)} fusion(s32[1,131072]{1,0:T(1,128)S(1)} %get-tuple-element.164, s32[4,131072]{1,0:T(4,128)S(1)} %get-tuple-element.187, s32[]{:T(128)S(6)} %copy.20), kind=kLoop, calls=%fused_computation.6.clone.1 | loop fusion | flops 1572864 | bytes 1572868 | tf_op jit(solution)/shard_map/while/body/eval_jaxpr/jit(floor_divide)/jit(_where)/select_n | solution.py:34
  90.4 1.1 iota_compare_fusion.4
  91.5 11.0 %select_reduce_fusion.2 = f32[4,131072]{1,0:T(4,128)S(1)} fusion(pred[16,131072]{1,0:T(8,128)(4,1)S(1)} %iota_compare_fusion.4, bf16[64,16]{0,1:T(8,128)(2,1)S(1)} %get-tuple-element.188, s32[131072]{0:T(1024)S(1)} %bitcast.60), kind=kOutput, calls=%fused_computation.clone.1 | convolution fusion | flops 286785536 | bytes 4720640 | tf_op jit(solution)/shard_map/while/body/eval_jaxpr/dot_general | solution.py:38
  102.5 1.6 %slice_reduce_fusion.2 = f32[131072]{0:T(1024)S(1)} fusion(f32[4,131072]{1,0:T(4,128)S(1)} %select_reduce_fusion.2), kind=kLoop, calls=%fused_computation.12.clone.1 | loop fusion | bytes 1048576 | tf_op jit(solution)/shard_map/while/body/eval_jaxpr/slice | solution.py:54
  104.4 0.6 reduce_sum.68
  105.1 2.9 %slice.46 = f32[3,2,65536]{2,1,0:T(2,128)} reshape(f32[3,131072]{1,0:T(4,128)S(1)} %bitcast.58) | data formatting | bytes 3145728 | tf_op jit(solution)/shard_map/while/body/eval_jaxpr/slice | solution.py:59
  108.0 1.1 reduce_window_sum.13
  109.0 0.7 exponential_multiply_fusion.2
  109.8 2.8 %multiply_reduce_fusion.2 = f32[3,65536]{1,0:T(4,128)S(1)} fusion(f32[3,2,65536]{2,1,0:T(2,128)S(1)} %copy-done.1, f32[2,65536]{1,0:T(2,128)S(1)} %exponential_multiply_fusion.2), kind=kLoop, calls=%fused_computation.7.clone.1 | loop fusion | flops 589824 | bytes 2883584 | tf_op jit(solution)/shard_map/while/body/eval_jaxpr/reduce_sum | solution.py:59
  112.6 0.6 select_add_fusion.2
  113.3 1.0 copy-done.3
  114.3 2.7 %pad_maximum_fusion = f32[1,4,256,256]{3,1,0,2:T(4,128)} fusion(f32[1,1,256,256]{3,1,0,2:T(1,128)S(1)} %bitcast.69, f32[1,3,256,256]{3,1,0,2:T(4,128)} %bitcast.61), kind=kLoop, calls=%fused_computation.17 | loop fusion | flops 262144 | bytes 2097152 | tf_op jit(solution)/shard_map/concatenate | solution.py:65
  116.9 5.2 %all-to-all-start = ((f32[1,4,256,256]{3,1,0,2:T(4,128)}), f32[1,4,256,256]{3,1,0,2:T(4,128)S(1)}, u32[]{:S(2)}, u32[]{:S(2)}) async-start(f32[1,4,256,256]{3,1,0,2:T(4,128)} %pad_maximum_fusion), calls=%async_computation | async-start | bytes 2097152 | tf_op jit(solution)/shard_map/all_to_all | solution.py:87
  122.4 13.4 %all-to-all-done = f32[1,4,256,256]{3,1,0,2:T(4,128)S(1)} async-done(((f32[1,4,256,256]{3,1,0,2:T(4,128)}), f32[1,4,256,256]{3,1,0,2:T(4,128)S(1)}, u32[]{:S(2)}, u32[]{:S(2)}) %all-to-all-start) | async-done | bytes 1048608 | tf_op jit(solution)/shard_map/all_to_all | solution.py:87
  135.8 0.7 copy.16
  136.8 0.6 fusion.2
  137.4 0.5 fusion.3
  138.1 1.7 %collective-permute-start.1 = (f32[1,4,8,256]{3,2,0,1:T(8,128)S(1)}, f32[1,4,8,256]{3,2,0,1:T(8,128)S(1)}, u32[]{:S(2)}, u32[]{:S(2)}) collective-permute-start(f32[1,4,8,256]{3,2,0,1:T(8,128)S(1)} %get-tuple-element.125), channel_id=1, source_target_pairs={{0,2},{1,3},{2,4},{3,5},{4,6},{5,7},{6,0},{7,1},{8,10},{9,11},{10,... | collective-permute-start | bytes 98312 | tf_op jit(solution)/shard_map/ppermute | solution.py:101
  139.7 2.5 %collective-permute-start.2 = (f32[1,4,8,256]{3,2,0,1:T(8,128)S(1)}, f32[1,4,8,256]{3,2,0,1:T(8,128)S(1)}, u32[]{:S(2)}, u32[]{:S(2)}) collective-permute-start(f32[1,4,8,256]{3,2,0,1:T(8,128)S(1)} %get-tuple-element.126), channel_id=1, source_target_pairs={{0,3},{1,4},{2,5},{3,6},{4,7},{5,0},{6,1},{7,2},{8,11},{9,12},{10,... | collective-permute-start | bytes 98312 | tf_op jit(solution)/shard_map/ppermute | solution.py:101
  142.3 1.2 collective-permute-start.3
  143.5 1.2 collective-permute-start.4
  144.7 1.3 collective-permute-start.5
  146.0 1.4 collective-permute-start.6
  147.6 1.0 collective-permute-done.5
  149.1 0.7 copy-done.6
  (78 shorter events, 3.0 us)
Async XLA Ops:
  0.0 122.1 %copy-start = (s32[8,4]{0,1:T(4,128)S(1)}, s32[8,4]{0,1:T(4,128)}, u32[]{:S(2)}) copy-start(s32[8,4]{0,1:T(4,128)} %param.9) | copy-start | bytes 388
  0.0 2.7 %copy-start.8 = (bf16[256]{0:T(256)(128)(2,1)S(1)}, bf16[256]{0:T(256)(128)(2,1)}, u32[]{:S(2)}) copy-start(bf16[256]{0:T(256)(128)(2,1)} %param.8) | copy-start | bytes 1540
  0.0 2.7 %copy-start.7 = (bf16[3,256]{1,0:T(4,128)(2,1)S(1)}, bf16[3,256]{1,0:T(4,128)(2,1)}, u32[]{:S(2)}) copy-start(bf16[3,256]{1,0:T(4,128)(2,1)} %param.7) | copy-start | bytes 4612
  2.9 5.1 %copy-start.4 = (s32[4,131072]{1,0:T(4,128)}, s32[4,131072]{1,0:T(4,128)S(1)}, u32[]{:S(2)}) copy-start(s32[4,131072]{1,0:T(4,128)S(1)} %get-tuple-element.187) | copy-start | bytes 6291460 | tf_op jit(solution)/shard_map/while
  24.5 1.8 %copy-start.1 = (f32[3,2,65536]{2,1,0:T(2,128)S(1)}, f32[3,2,65536]{2,1,0:T(2,128)}, u32[]{:S(2)}) copy-start(f32[3,2,65536]{2,1,0:T(2,128)} %slice.46) | copy-start | bytes 4718596 | tf_op jit(solution)/shard_map/while
  25.6 3.6 %copy-start.2 = (f32[3,65536]{1,0:T(4,128)S(1)}, f32[3,65536]{1,0:T(4,128)}, u32[]{:S(2)}) copy-start(f32[3,65536]{1,0:T(4,128)} %get-tuple-element.178) | copy-start | bytes 2359300 | tf_op jit(solution)/shard_map/while
  29.1 1.6 %copy-start.5 = (s32[4,131072]{1,0:T(4,128)S(1)}, s32[4,131072]{1,0:T(4,128)}, u32[]{:S(2)}) copy-start(s32[4,131072]{1,0:T(4,128)} %copy-done.4) | copy-start | bytes 6291460 | tf_op jit(solution)/shard_map/while
  29.8 1.0 copy-start.3
  30.7 5.1 %copy-start.4 = (s32[4,131072]{1,0:T(4,128)}, s32[4,131072]{1,0:T(4,128)S(1)}, u32[]{:S(2)}) copy-start(s32[4,131072]{1,0:T(4,128)S(1)} %get-tuple-element.187) | copy-start | bytes 6291460 | tf_op jit(solution)/shard_map/while
  52.3 1.8 %copy-start.1 = (f32[3,2,65536]{2,1,0:T(2,128)S(1)}, f32[3,2,65536]{2,1,0:T(2,128)}, u32[]{:S(2)}) copy-start(f32[3,2,65536]{2,1,0:T(2,128)} %slice.46) | copy-start | bytes 4718596 | tf_op jit(solution)/shard_map/while
  53.4 3.6 %copy-start.2 = (f32[3,65536]{1,0:T(4,128)S(1)}, f32[3,65536]{1,0:T(4,128)}, u32[]{:S(2)}) copy-start(f32[3,65536]{1,0:T(4,128)} %get-tuple-element.178) | copy-start | bytes 2359300 | tf_op jit(solution)/shard_map/while
  57.0 1.6 %copy-start.5 = (s32[4,131072]{1,0:T(4,128)S(1)}, s32[4,131072]{1,0:T(4,128)}, u32[]{:S(2)}) copy-start(s32[4,131072]{1,0:T(4,128)} %copy-done.4) | copy-start | bytes 6291460 | tf_op jit(solution)/shard_map/while
  57.6 1.0 copy-start.3
  58.6 5.1 %copy-start.4 = (s32[4,131072]{1,0:T(4,128)}, s32[4,131072]{1,0:T(4,128)S(1)}, u32[]{:S(2)}) copy-start(s32[4,131072]{1,0:T(4,128)S(1)} %get-tuple-element.187) | copy-start | bytes 6291460 | tf_op jit(solution)/shard_map/while
  80.1 1.8 %copy-start.1 = (f32[3,2,65536]{2,1,0:T(2,128)S(1)}, f32[3,2,65536]{2,1,0:T(2,128)}, u32[]{:S(2)}) copy-start(f32[3,2,65536]{2,1,0:T(2,128)} %slice.46) | copy-start | bytes 4718596 | tf_op jit(solution)/shard_map/while
  81.2 3.6 %copy-start.2 = (f32[3,65536]{1,0:T(4,128)S(1)}, f32[3,65536]{1,0:T(4,128)}, u32[]{:S(2)}) copy-start(f32[3,65536]{1,0:T(4,128)} %get-tuple-element.178) | copy-start | bytes 2359300 | tf_op jit(solution)/shard_map/while
  84.8 1.6 %copy-start.5 = (s32[4,131072]{1,0:T(4,128)S(1)}, s32[4,131072]{1,0:T(4,128)}, u32[]{:S(2)}) copy-start(s32[4,131072]{1,0:T(4,128)} %copy-done.4) | copy-start | bytes 6291460 | tf_op jit(solution)/shard_map/while
  85.4 1.0 copy-start.3
  86.4 5.1 %copy-start.4 = (s32[4,131072]{1,0:T(4,128)}, s32[4,131072]{1,0:T(4,128)S(1)}, u32[]{:S(2)}) copy-start(s32[4,131072]{1,0:T(4,128)S(1)} %get-tuple-element.187) | copy-start | bytes 6291460 | tf_op jit(solution)/shard_map/while
  108.0 1.8 %copy-start.1 = (f32[3,2,65536]{2,1,0:T(2,128)S(1)}, f32[3,2,65536]{2,1,0:T(2,128)}, u32[]{:S(2)}) copy-start(f32[3,2,65536]{2,1,0:T(2,128)} %slice.46) | copy-start | bytes 4718596 | tf_op jit(solution)/shard_map/while
  109.0 3.6 %copy-start.2 = (f32[3,65536]{1,0:T(4,128)S(1)}, f32[3,65536]{1,0:T(4,128)}, u32[]{:S(2)}) copy-start(f32[3,65536]{1,0:T(4,128)} %get-tuple-element.178) | copy-start | bytes 2359300 | tf_op jit(solution)/shard_map/while
  112.6 1.6 %copy-start.5 = (s32[4,131072]{1,0:T(4,128)S(1)}, s32[4,131072]{1,0:T(4,128)}, u32[]{:S(2)}) copy-start(s32[4,131072]{1,0:T(4,128)} %copy-done.4) | copy-start | bytes 6291460 | tf_op jit(solution)/shard_map/while
  113.2 1.0 copy-start.3
  116.9 18.8 %all-to-all-start = ((f32[1,4,256,256]{3,1,0,2:T(4,128)}), f32[1,4,256,256]{3,1,0,2:T(4,128)S(1)}, u32[]{:S(2)}, u32[]{:S(2)}) async-start(f32[1,4,256,256]{3,1,0,2:T(4,128)} %pad_maximum_fusion), calls=%async_computation | async-start | bytes 2097152 | tf_op jit(solution)/shard_map/all_to_all | solution.py:87
  138.0 6.7 %collective-permute-start = (f32[1,4,8,256]{3,2,0,1:T(8,128)S(1)}, f32[1,4,8,256]{3,2,0,1:T(8,128)S(1)}, u32[]{:S(2)}, u32[]{:S(2)}) collective-permute-start(f32[1,4,8,256]{3,2,0,1:T(8,128)S(1)} %get-tuple-element.124), channel_id=1, source_target_pairs={{0,1},{1,2},{2,3},{3,4},{4,5},{5,6},{6,7},{7,0},{8,9},{9,10},{10,1... | collective-permute-start | bytes 98312 | tf_op jit(solution)/shard_map/ppermute | solution.py:101
  138.1 8.0 %collective-permute-start.1 = (f32[1,4,8,256]{3,2,0,1:T(8,128)S(1)}, f32[1,4,8,256]{3,2,0,1:T(8,128)S(1)}, u32[]{:S(2)}, u32[]{:S(2)}) collective-permute-start(f32[1,4,8,256]{3,2,0,1:T(8,128)S(1)} %get-tuple-element.125), channel_id=1, source_target_pairs={{0,2},{1,3},{2,4},{3,5},{4,6},{5,7},{6,0},{7,1},{8,10},{9,11},{10,... | collective-permute-start | bytes 98312 | tf_op jit(solution)/shard_map/ppermute | solution.py:101
  139.7 7.8 %collective-permute-start.2 = (f32[1,4,8,256]{3,2,0,1:T(8,128)S(1)}, f32[1,4,8,256]{3,2,0,1:T(8,128)S(1)}, u32[]{:S(2)}, u32[]{:S(2)}) collective-permute-start(f32[1,4,8,256]{3,2,0,1:T(8,128)S(1)} %get-tuple-element.126), channel_id=1, source_target_pairs={{0,3},{1,4},{2,5},{3,6},{4,7},{5,0},{6,1},{7,2},{8,11},{9,12},{10,... | collective-permute-start | bytes 98312 | tf_op jit(solution)/shard_map/ppermute | solution.py:101
  142.3 5.3 %collective-permute-start.3 = (f32[1,4,8,256]{3,2,0,1:T(8,128)S(1)}, f32[1,4,8,256]{3,2,0,1:T(8,128)S(1)}, u32[]{:S(2)}, u32[]{:S(2)}) collective-permute-start(f32[1,4,8,256]{3,2,0,1:T(8,128)S(1)} %get-tuple-element.127), channel_id=1, source_target_pairs={{0,4},{1,5},{2,6},{3,7},{4,0},{5,1},{6,2},{7,3},{8,12},{9,13},{10,... | collective-permute-start | bytes 98312 | tf_op jit(solution)/shard_map/ppermute | solution.py:101
  143.5 4.1 %collective-permute-start.4 = (f32[1,4,8,256]{3,2,0,1:T(8,128)S(1)}, f32[1,4,8,256]{3,2,0,1:T(8,128)S(1)}, u32[]{:S(2)}, u32[]{:S(2)}) collective-permute-start(f32[1,4,8,256]{3,2,0,1:T(8,128)S(1)} %get-tuple-element.128), channel_id=1, source_target_pairs={{0,5},{1,6},{2,7},{3,0},{4,1},{5,2},{6,3},{7,4},{8,13},{9,14},{10,... | collective-permute-start | bytes 98312 | tf_op jit(solution)/shard_map/ppermute | solution.py:101
  144.7 3.9 %collective-permute-start.5 = (f32[1,4,8,256]{3,2,0,1:T(8,128)S(1)}, f32[1,4,8,256]{3,2,0,1:T(8,128)S(1)}, u32[]{:S(2)}, u32[]{:S(2)}) collective-permute-start(f32[1,4,8,256]{3,2,0,1:T(8,128)S(1)} %fusion.20), channel_id=1, source_target_pairs={{0,6},{1,7},{2,0},{3,1},{4,2},{5,3},{6,4},{7,5},{8,14},{9,15},{10,... | collective-permute-start | bytes 98312 | tf_op jit(solution)/shard_map/ppermute | solution.py:101
  146.0 3.0 %collective-permute-start.6 = (f32[1,4,8,256]{3,2,0,1:T(8,128)S(1)}, f32[1,4,8,256]{3,2,0,1:T(8,128)S(1)}, u32[]{:S(2)}, u32[]{:S(2)}) collective-permute-start(f32[1,4,8,256]{3,2,0,1:T(8,128)S(1)} %get-tuple-element.123), channel_id=1, source_target_pairs={{0,7},{1,0},{2,1},{3,2},{4,3},{5,4},{6,5},{7,6},{8,15},{9,8},{10,9... | collective-permute-start | bytes 98312 | tf_op jit(solution)/shard_map/ppermute | solution.py:101
  149.1 0.7 copy-start.6
